TPU v7x, 128 devices: a whole 4x4x4 slice. The times are simulated.
128 devices in a mesh: dp: 8 (over x, y_hi), expert: 16 (over z, y_lo, core).
Axes of the slice: x: 4, y: 4 (y_hi: 2, y_lo: 2; y = y_hi * 2 + y_lo), z: 4, core: 2. Of those that a mesh axis runs over, the one named last changes fastest.
Arguments:
- tokens: bfloat16 [16384, 4096], P(('dp', 'expert')), may hold values from -6 to 6
- cotangent: bfloat16 [16384, 4096], P(('dp', 'expert')), may hold values from -3 to 3
- expert_ids: int32 [16384, 8, 2], P(('dp', 'expert')), may hold values from 0 to 31, as said below
- slot_ids: int32 [16384, 8, 2], P(('dp', 'expert')), may hold values from 0 to 63, as said below
- route_probs: bfloat16 [16384, 8, 2], P(('dp', 'expert')), may hold values from 0.099609375 to 1
- weights_in: bfloat16 [32, 2, 1792, 512], P('expert', None, 'dp'), may hold values from -0.25 to 0.25
- weights_out: bfloat16 [32, 1792, 512], P('expert', 'dp'), may hold values from -0.125 to 0.125
Outputs:
- grad_tokens: bfloat16 [16384, 4096], P(('dp', 'expert'))
- grad_probs: float32 [16384, 8, 2], P(('dp', 'expert'))
- grad_in: bfloat16 [32, 2, 1792, 512], P('expert', None, 'dp')
- grad_out: bfloat16 [32, 1792, 512], P('expert', 'dp')
Inputs may be any that keep to these rules, and one draw needn't show every extreme that they name: `expert_ids`: each sub-token names 2 different experts. On each device the experts fall into two sets of 16, and the two ids of a sub-token come one from each set. Every expert is named by exactly 64 sub-tokens of every device. `slot_ids`: for each device and expert, the sub-tokens of that device that name the expert carry distinct slot numbers at the matching position.
All inputs are finite; a program needn't handle non-finite values.
Results may differ from a plain program's by a relative error of at most 0.012.
Values may be sent and summed in bfloat16 or wider, within the bound.
No kernel may reach another device: no remote copies, remote signals or barrier semaphores. Data moves between devices by JAX's collectives and lax.ppermute only.
A program may use at most 192 MiB of HBM per device.

v0:
```python
import math
import jax
import jax.numpy as jnp
from jax import lax
from jax.sharding import PartitionSpec as P

H = 8
DS = 512


def side_by_side(arrays, axis, split_dim, concat_dim, along):
    widths = [math.prod(a.shape[along:]) for a in arrays]
    both = jnp.concatenate(
        [a.reshape(*a.shape[:along], w) for a, w in zip(arrays, widths)], axis=along
    )
    filled = lax.all_to_all(both, axis, split_axis=split_dim, concat_axis=concat_dim, tiled=True)
    tiles = jnp.split(filled, [sum(widths[:k]) for k in range(1, len(widths))], axis=along)
    return tuple(
        (b.reshape(*filled.shape[:along], *a.shape[along:]) for a, b in zip(arrays, tiles))
    )


def rows_first(arrays, axis, dims):
    turned = [jnp.moveaxis(a, dim, 0) for a, dim in zip(arrays, dims)]
    widths = [t[0].size for t in turned]
    both = jnp.concatenate([t.reshape(-1, w) for t, w in zip(turned, widths)], axis=1)
    filled = lax.all_gather(both, axis, axis=0, tiled=True)
    tiles = jnp.split(filled, [sum(widths[:k]) for k in range(1, len(widths))], axis=1)
    return tuple(
        (
            jnp.moveaxis(b.reshape(-1, *t.shape[1:]), 0, dim)
            for b, t, dim in zip(tiles, turned, dims)
        )
    )


def contract_last(former, latter):
    return lax.dot_general(
        former, latter, (((1,), (1,)), ((), ())), preferred_element_type=jnp.float32
    )


def expert_backward(inputs, cotangent, weighting, gate_up, down_proj):
    gate_pre = contract_last(inputs, gate_up[0])
    up_pre = contract_last(inputs, gate_up[1])
    sigmoids = jax.nn.sigmoid(gate_pre)
    activated = gate_pre * sigmoids
    hidden = (activated * up_pre).astype(jnp.bfloat16)
    output = jnp.dot(hidden, down_proj, preferred_element_type=jnp.float32)
    router_grad = jnp.sum(output * cotangent.astype(jnp.float32), axis=1).astype(jnp.bfloat16)
    scaled = (weighting.astype(jnp.float32)[:, None] * cotangent.astype(jnp.float32)).astype(
        jnp.bfloat16
    )
    dhidden = contract_last(scaled, down_proj)
    gate_grad = (dhidden * up_pre * sigmoids * (1.0 + gate_pre * (1.0 - sigmoids))).astype(
        jnp.bfloat16
    )
    up_grad = (dhidden * activated).astype(jnp.bfloat16)
    input_grad = jnp.dot(gate_grad, gate_up[0], preferred_element_type=jnp.float32)
    input_grad = (
        input_grad + jnp.dot(up_grad, gate_up[1], preferred_element_type=jnp.float32)
    ).astype(jnp.bfloat16)
    return (input_grad, router_grad, gate_grad, up_grad, hidden, scaled)


def reduce_grads(inputs, gate_grad, up_grad, hidden, scaled):
    gate_term = jnp.einsum("rf,rd->fd", gate_grad, inputs, preferred_element_type=jnp.float32)
    up_term = jnp.einsum("rf,rd->fd", up_grad, inputs, preferred_element_type=jnp.float32)
    summed = lax.psum_scatter(
        jnp.concatenate(
            [
                jnp.stack([gate_term, up_term], axis=1),
                jnp.einsum("rf,rd->fd", hidden, scaled, preferred_element_type=jnp.float32)[
                    :, None, :
                ],
            ],
            axis=1,
        ).astype(jnp.bfloat16),
        "dp",
        scatter_dimension=0,
        tiled=True,
    ).astype(jnp.float32)
    pair_sum = summed[:, :2]
    down_sum = summed[:, 2]
    return (jnp.transpose(pair_sum, (1, 0, 2)).astype(jnp.bfloat16), down_sum.astype(jnp.bfloat16))


def body(tokens, cotangent, expert_ids, slot_ids, route_probs, weights_in, weights_out):
    peers = lax.axis_size("expert")
    local_count = weights_in.shape[0]
    token_count = tokens.shape[0]
    sub_count = token_count * H
    capacity = sub_count * 2 // (local_count * peers)
    buffer_rows = local_count * peers * capacity
    chosen = expert_ids.reshape(sub_count, 2)
    placed = (
        chosen % local_count * (peers * capacity)
        + chosen // local_count * capacity
        + slot_ids.reshape(sub_count, 2)
    )
    flat_place = placed.reshape(-1)

    def spread(values):
        doubled = jnp.broadcast_to(values[:, None, :], (sub_count, 2, DS)).reshape(
            2 * sub_count, DS
        )
        filled = jnp.zeros((buffer_rows, DS), jnp.bfloat16).at[flat_place].set(doubled)
        return filled.reshape(local_count, peers, capacity, DS)

    input_buffer = spread(tokens.reshape(sub_count, DS))
    cotangent_buffer = spread(cotangent.reshape(sub_count, DS))
    prob_buffer = (
        jnp.zeros((buffer_rows,), jnp.bfloat16).at[flat_place].set(route_probs.reshape(-1))
    )
    prob_buffer = prob_buffer.reshape(local_count, peers, capacity)
    arrived_in = lax.all_to_all(input_buffer, "expert", split_axis=1, concat_axis=1, tiled=True)
    arrived_cot, arrived_prob = side_by_side((cotangent_buffer, prob_buffer), "expert", 1, 1, 3)
    input_grads = []
    router_grads = []
    grads_pair = []
    grads_down = []
    for expert_pos in range(local_count):
        single_in, single_out = rows_first(
            (weights_in[expert_pos : expert_pos + 1], weights_out[expert_pos : expert_pos + 1]),
            "dp",
            (2, 1),
        )
        gate_up = single_in[0]
        down_proj = single_out[0]
        rows_in = arrived_in[expert_pos].reshape(peers * capacity, DS)
        rows_cot = arrived_cot[expert_pos].reshape(peers * capacity, DS)
        rows_prob = arrived_prob[expert_pos].reshape(peers * capacity)
        input_grad, router_grad, gate_grad, up_grad, hidden, scaled = expert_backward(
            rows_in, rows_cot, rows_prob, gate_up, down_proj
        )
        pair_part, down_part = reduce_grads(rows_in, gate_grad, up_grad, hidden, scaled)
        input_grads.append(input_grad)
        router_grads.append(router_grad)
        grads_pair.append(pair_part)
        grads_down.append(down_part)
    stacked_inputs = jnp.stack(input_grads).reshape(local_count, peers, capacity, DS)
    stacked_router = jnp.stack(router_grads).reshape(local_count, peers, capacity)
    returned, returned_router = side_by_side((stacked_inputs, stacked_router), "expert", 1, 1, 3)
    back_rows = (
        returned.reshape(buffer_rows, DS)[flat_place].reshape(sub_count, 2, DS).astype(jnp.float32)
    )
    grad_tokens = jnp.sum(back_rows, axis=1).astype(jnp.bfloat16).reshape(token_count, H * DS)
    grad_probs = (
        returned_router.reshape(buffer_rows)[flat_place]
        .reshape(token_count, H, 2)
        .astype(jnp.float32)
    )
    return (grad_tokens, grad_probs, jnp.stack(grads_pair), jnp.stack(grads_down))


def solution(mesh):
    return jax.shard_map(
        body,
        mesh=mesh,
        in_specs=(
            P(("dp", "expert"), None),
            P(("dp", "expert"), None),
            P(("dp", "expert"), None, None),
            P(("dp", "expert"), None, None),
            P(("dp", "expert"), None, None),
            P("expert", None, "dp", None),
            P("expert", "dp", None),
        ),
        out_specs=(
            P(("dp", "expert"), None),
            P(("dp", "expert"), None, None),
            P("expert", None, "dp", None),
            P("expert", "dp", None),
        ),
        check_vma=False,
    )
```

profile of v0, /device:TPU:0, one launch (start us, length us, event | category | flops | bytes accessed | tf_op | source)
XLA Modules:
  0.0 402.9 jit_solution(530225747279303801)
XLA Ops:
  15.4 2.2 reshape.320
  17.7 10.6 %scatter_custom_fusion.2 = bf16[2048,512]{1,0:T(8,128)(2,1)S(1)} fusion(s32[2048]{0:T(1024)S(1)} %bitcast.149, bf16[2048,512]{1,0:T(8,128)(2,1)} %reshape.320, bf16[]{:T(256)} %constant.31.clone.1), kind=kCustom, calls=%fused_computation.59 | custom fusion | bytes 2097664 | tf_op jit(solution)/shard_map/scatter | solution.py:107
  29.8 6.8 %all-to-all-start.1 = ((bf16[2,16,64,512]{3,2,0,1:T(8,128)(2,1)}), bf16[2,16,64,512]{3,2,0,1:T(8,128)(2,1)S(1)}, u32[]{:S(2)}, u32[]{:S(2)}) async-start(bf16[2,16,64,512]{3,2,0,1:T(8,128)(2,1)} %copy.47), calls=%async_computation.1 | async-start | bytes 4194304 | tf_op jit(solution)/shard_map/all_to_all | solution.py:116
  37.1 14.6 %scatter_custom_fusion.1 = bf16[2048]{0:T(1024)(128)(2,1)S(1)} fusion(s32[2048]{0:T(1024)S(1)} %bitcast.150, bf16[2048]{0:T(1024)(128)(2,1)S(1)} %reshape.312, bf16[]{:T(256)} %constant.31.clone.1), kind=kCustom, calls=%fused_computation.88 | custom fusion | bytes 4098 | tf_op jit(solution)/shard_map/scatter | solution.py:113
  55.1 2.4 broadcast_in_dim.33
  57.5 4.2 %reshape.304 = bf16[2048,512]{1,0:T(8,128)(2,1)} reshape(bf16[1024,2,512]{2,1,0:T(2,128)(2,1)} %broadcast_in_dim.33) | data formatting | bytes 4194304 | tf_op jit(solution)/shard_map/reshape | solution.py:104
  61.7 11.5 %scatter_custom_fusion = bf16[2048,512]{1,0:T(8,128)(2,1)} fusion(s32[2048]{0:T(1024)S(1)} %bitcast.151, bf16[2048,512]{1,0:T(8,128)(2,1)} %reshape.304, bf16[]{:T(256)} %constant.31.clone.1), kind=kCustom, calls=%fused_computation.61 | custom fusion | bytes 2097664 | tf_op jit(solution)/shard_map/scatter | solution.py:107
  73.2 2.0 pad_maximum_fusion.2
  78.3 5.8 %all-to-all-start = ((bf16[2,16,64,513]{3,2,0,1:T(8,128)(2,1)}), bf16[2,16,64,513]{3,2,0,1:T(8,128)(2,1)S(1)}, u32[]{:S(2)}, u32[]{:S(2)}) async-start(bf16[2,16,64,513]{3,2,0,1:T(8,128)(2,1)} %copy.44), calls=%async_computation | async-start | bytes 5242880 | tf_op jit(solution)/shard_map/all_to_all | solution.py:16
  84.2 3.1 fusion.32
  87.3 35.7 %all-to-all-done = bf16[2,16,64,513]{3,2,0,1:T(8,128)(2,1)S(1)} async-done(((bf16[2,16,64,513]{3,2,0,1:T(8,128)(2,1)}), bf16[2,16,64,513]{3,2,0,1:T(8,128)(2,1)S(1)}, u32[]{:S(2)}, u32[]{:S(2)}) %all-to-all-start) | async-done | bytes 2101280 | tf_op jit(solution)/shard_map/all_to_all | solution.py:16
  125.9 4.2 %split.29 = bf16[1792,1024]{1,0:T(8,128)(2,1)} slice(bf16[1792,1536]{1,0:T(8,128)(2,1)} %all-gather.5.cloned.1.call-done), slice={[0:1792], [0:1024]} | slice | bytes 7340032 | tf_op jit(solution)/shard_map/split | solution.py:28
  130.1 7.6 %reshape.275 = bf16[1792,1,2,512]{3,2,0,1:T(2,128)(2,1)} reshape(bf16[1792,1024]{1,0:T(8,128)(2,1)} %split.29) | data formatting | bytes 7340032 | tf_op jit(solution)/shard_map/reshape | solution.py:31
  137.8 2.7 copy.66
  140.5 2.1 fusion.13
  142.6 6.6 %fusion.17 = f32[1024,1792]{1,0:T(8,128)} fusion(bf16[1024,512]{1,0:T(8,128)(2,1)S(1)} %multiply_convert_fusion.6, bf16[1792,1536]{1,0:T(8,128)(2,1)} %all-gather.5.cloned.1.call-done), kind=kOutput, calls=%fused_computation.52 | convolution fusion | flops 1879048192 | bytes 10223616 | tf_op jit(solution)/shard_map/dot_general | solution.py:38
  149.3 9.4 %multiply_convert_fusion.3 = (bf16[1024,1792]{1,0:T(8,128)(2,1)S(1)}, bf16[1024,1792]{1,0:T(8,128)(2,1)}, bf16[1024,1792]{1,0:T(8,128)(2,1)}) fusion(f32[1024,1792]{1,0:T(8,128)} %fusion.17, f32[1024,1792]{1,0:T(8,128)S(1)} %fusion.13, bf16[1024,512]{1,0:T(8,128)(2,1)S(1)} %bitcast.146, bf16[1,2,1792,512]{3,2,1,0:T(8,128)(2,1)S(1)} %bitcast.128), kind=kOutput, calls=%fused_computation.8 | convolution fusion | flops 1906573312 | bytes 28573696 | tf_op jit(solution)/shard_map/dot_general | solution.py:38
  158.7 5.5 %fusion.7 = bf16[1792,1,512]{2,0,1:T(8,128)(2,1)S(1)} fusion(bf16[1024,1792]{1,0:T(8,128)(2,1)} %get-tuple-element.22, bf16[1024,512]{1,0:T(8,128)(2,1)S(1)} %multiply_convert_fusion.6), kind=kOutput, calls=%fused_computation.30 | convolution fusion | flops 1879965696 | bytes 6553600 | tf_op jit(solution)/shard_map/rf,rd->fd/dot_general | solution.py:73
  164.3 2.1 fusion.6
  166.4 2.1 fusion.5
  168.6 3.0 pad_maximum_fusion.1
  173.1 21.6 %all-gather.3.cloned.1.call-done = bf16[1792,1536]{1,0:T(8,128)(2,1)} async-done(((bf16[224,1536]{1,0:T(8,128)(2,1)}), bf16[1792,1536]{1,0:T(8,128)(2,1)}) %all-gather.3.cloned.1.call-update) | async-done | bytes 5505040 | tf_op jit(solution)/shard_map/all_gather | solution.py:27
  194.7 4.2 %split.27 = bf16[1792,1024]{1,0:T(8,128)(2,1)} slice(bf16[1792,1536]{1,0:T(8,128)(2,1)} %all-gather.3.cloned.1.call-done), slice={[0:1792], [0:1024]} | slice | bytes 7340032 | tf_op jit(solution)/shard_map/split | solution.py:28
  198.9 7.3 %reshape.273 = bf16[1792,1,2,512]{3,2,0,1:T(2,128)(2,1)} reshape(bf16[1792,1024]{1,0:T(8,128)(2,1)} %split.27) | data formatting | bytes 7340032 | tf_op jit(solution)/shard_map/reshape | solution.py:31
  206.2 2.7 copy.67
  208.9 2.1 fusion.9
  211.0 6.5 %fusion.20 = f32[1024,1792]{1,0:T(8,128)} fusion(bf16[1024,512]{1,0:T(8,128)(2,1)S(1)} %multiply_convert_fusion.7, bf16[1792,1536]{1,0:T(8,128)(2,1)} %all-gather.3.cloned.1.call-done), kind=kOutput, calls=%fused_computation.55 | convolution fusion | flops 1879048192 | bytes 10223616 | tf_op jit(solution)/shard_map/dot_general | solution.py:38
  217.6 9.6 %multiply_convert_fusion.5 = (bf16[1024,1792]{1,0:T(8,128)(2,1)S(1)}, bf16[1024,1792]{1,0:T(8,128)(2,1)}, bf16[1024,1792]{1,0:T(8,128)(2,1)}) fusion(f32[1024,1792]{1,0:T(8,128)} %fusion.20, f32[1024,1792]{1,0:T(8,128)S(1)} %fusion.9, bf16[1024,512]{1,0:T(8,128)(2,1)S(1)} %bitcast.142, bf16[1,2,1792,512]{3,2,1,0:T(8,128)(2,1)S(1)} %bitcast.132), kind=kOutput, calls=%fused_computation.12 | convolution fusion | flops 1906573312 | bytes 28573696 | tf_op jit(solution)/shard_map/dot_general | solution.py:38
  227.2 5.5 %fusion.4 = bf16[1792,1,512]{2,0,1:T(8,128)(2,1)S(1)} fusion(bf16[1024,1792]{1,0:T(8,128)(2,1)} %get-tuple-element.19, bf16[1024,512]{1,0:T(8,128)(2,1)S(1)} %multiply_convert_fusion.7), kind=kOutput, calls=%fused_computation.27 | convolution fusion | flops 1879965696 | bytes 6553600 | tf_op jit(solution)/shard_map/rf,rd->fd/dot_general | solution.py:73
  232.7 2.1 fusion.3
  234.9 2.1 fusion.2
  237.0 2.9 pad_maximum_fusion
  242.9 3.1 copy.55
  248.2 5.7 %multiply_reduce_fusion = bf16[1024]{0:T(1024)(128)(2,1)S(1)} fusion(f32[1024,512]{0,1:T(8,128)} %copy.55, bf16[1024,1792]{1,0:T(8,128)(2,1)} %get-tuple-element.22, bf16[1792,1536]{1,0:T(8,128)(2,1)} %all-gather.5.cloned.1.call-done), kind=kOutput, calls=%fused_computation.33 | convolution fusion | flops 1880095744 | bytes 7604224 | tf_op jit(solution)/shard_map/dot_general | solution.py:49
  253.9 4.7 %multiply_reduce_fusion.1 = bf16[1024]{0:T(1024)(128)(2,1)S(1)} fusion(f32[1024,512]{0,1:T(8,128)S(1)} %copy-done.10, bf16[1024,1792]{1,0:T(8,128)(2,1)} %get-tuple-element.19, bf16[1792,1536]{1,0:T(8,128)(2,1)} %all-gather.3.cloned.1.call-done), kind=kOutput, calls=%fused_computation.34 | convolution fusion | flops 1880095744 | bytes 7604224 | tf_op jit(solution)/shard_map/dot_general | solution.py:49
  259.1 4.8 %fusion.12 = f32[1024,512]{1,0:T(8,128)S(1)} fusion(bf16[1024,1792]{1,0:T(8,128)(2,1)} %get-tuple-element.23, bf16[1,2,1792,512]{3,2,1,0:T(8,128)(2,1)} %bitcast.129), kind=kOutput, calls=%fused_computation.47 | convolution fusion | flops 1879048192 | bytes 7602176 | tf_op jit(solution)/shard_map/dot_general | solution.py:61
  264.0 2.0 fusion.8
  267.1 2.0 add_convert_fusion
  269.2 2.1 add_convert_fusion.1
  271.2 1.9 pad_maximum_fusion.3
  273.1 5.2 %all-to-all-start.2 = ((bf16[2,16,64,513]{3,2,0,1:T(8,128)(2,1)}), bf16[2,16,64,513]{3,2,0,1:T(8,128)(2,1)S(1)}, u32[]{:S(2)}, u32[]{:S(2)}) async-start(bf16[2,16,64,513]{3,2,0,1:T(8,128)(2,1)} %pad_maximum_fusion.3), calls=%async_computation.2 | async-start | bytes 5242880 | tf_op jit(solution)/shard_map/all_to_all | solution.py:16
  278.3 39.6 %all-to-all-done.2 = bf16[2,16,64,513]{3,2,0,1:T(8,128)(2,1)S(1)} async-done(((bf16[2,16,64,513]{3,2,0,1:T(8,128)(2,1)}), bf16[2,16,64,513]{3,2,0,1:T(8,128)(2,1)S(1)}, u32[]{:S(2)}, u32[]{:S(2)}) %all-to-all-start.2) | async-done | bytes 2101280 | tf_op jit(solution)/shard_map/all_to_all | solution.py:16
  319.8 9.2 %gather_fusion = bf16[2048,512]{1,0:T(8,128)(2,1)} fusion(bf16[2048,512]{1,0:T(8,128)(2,1)S(1)} %bitcast.124, s32[2048]{0:T(1024)S(1)} %broadcast_clamp_fusion), kind=kCustom, calls=%fused_computation | custom fusion | bytes 4202496 | tf_op jit(solution)/shard_map/gather | solution.py:145
  329.0 2.8 reshape.277
  331.8 6.7 %reduce_sum.32 = bf16[1024,512]{1,0:T(8,128)(2,1)} reduce(bf16[1024,2,512]{2,1,0:T(2,128)(2,1)S(1)} %reshape.277, bf16[]{:T(256)} %constant.31.clone.1), dimensions={1}, to_apply=%region_5.6 | reduce | flops 524288 | bytes 3145730 | tf_op jit(solution)/shard_map/reduce_sum | solution.py:147
  338.5 2.3 reshape.278
  341.2 13.1 %gather_fusion.1 = bf16[2048]{0:T(1024)(128)(2,1)S(1)} fusion(bf16[2048]{0:T(1024)(128)(2,1)S(1)} %reshape_reshape.8, s32[2048]{0:T(1024)S(1)} %broadcast_clamp_fusion), kind=kCustom, calls=%fused_computation.1 | custom fusion | bytes 16384 | tf_op jit(solution)/shard_map/gather | solution.py:149
  356.6 34.6 %reduce-scatter.3.cloned.1.call-done = bf16[224,3,512]{2,0,1:T(8,128)(2,1)} async-done(((bf16[1792,3,512]{2,0,1:T(8,128)(2,1)}), bf16[224,3,512]{2,0,1:T(8,128)(2,1)}) %reduce-scatter.3.cloned.1.call-update) | async-done | bytes 688144 | tf_op jit(solution)/shard_map/reduce_scatter | solution.py:69
  (108 shorter events, 37.3 us)
Async XLA Ops:
  7.2 118.8 %all-gather.5.cloned.1.call-start = ((), (), s32[]{:S(2)}) async-start(), calls=%async_computation.6 | async-start | bytes 6193152 | tf_op jit(solution)/shard_map/all_gather | solution.py:27
  10.0 2.5 copy-start.14
  10.1 3.0 copy-start.15
  11.0 2.8 copy-start.11
  11.0 183.6 %all-gather.3.cloned.1.call-start = ((), (), s32[]{:S(2)}) async-start(), calls=%async_computation.5 | async-start | bytes 6193152 | tf_op jit(solution)/shard_map/all_gather | solution.py:27
  28.3 8.3 %copy-start.16 = (bf16[128,8,2]{0,2,1:T(2,128)(2,1)S(1)}, bf16[128,8,2]{0,2,1:T(2,128)(2,1)}, u32[]{:S(2)}) copy-start(bf16[128,8,2]{0,2,1:T(2,128)(2,1)} %param.11) | copy-start | bytes 12292
  29.8 47.2 %all-to-all-start.1 = ((bf16[2,16,64,512]{3,2,0,1:T(8,128)(2,1)}), bf16[2,16,64,512]{3,2,0,1:T(8,128)(2,1)S(1)}, u32[]{:S(2)}, u32[]{:S(2)}) async-start(bf16[2,16,64,512]{3,2,0,1:T(8,128)(2,1)} %copy.47), calls=%async_computation.1 | async-start | bytes 4194304 | tf_op jit(solution)/shard_map/all_to_all | solution.py:116
  57.5 15.7 %copy-start.9 = (bf16[2,16,64,1]{3,2,1,0:T(8,128)(2,1)S(1)}, bf16[2,16,64,1]{3,2,1,0:T(8,128)(2,1)}, u32[]{:S(2)}) copy-start(bf16[2,16,64,1]{3,2,1,0:T(8,128)(2,1)} %reshape_reshape.9) | copy-start | bytes 12292
  77.0 1.4 copy-start.4
  78.3 44.7 %all-to-all-start = ((bf16[2,16,64,513]{3,2,0,1:T(8,128)(2,1)}), bf16[2,16,64,513]{3,2,0,1:T(8,128)(2,1)S(1)}, u32[]{:S(2)}, u32[]{:S(2)}) async-start(bf16[2,16,64,513]{3,2,0,1:T(8,128)(2,1)} %copy.44), calls=%async_computation | async-start | bytes 5242880 | tf_op jit(solution)/shard_map/all_to_all | solution.py:16
  84.1 271.5 %reduce-scatter.5.cloned.1.call-start = ((), (), s32[]{:S(2)}) async-start(), calls=%async_computation.8 | async-start | bytes 6193152 | tf_op jit(solution)/shard_map/reduce_scatter | solution.py:69
  124.6 1.0 copy-start.2
  137.8 2.8 copy-start.13
  140.5 8.8 %copy-start.5 = (bf16[1792,1,2,512]{3,0,2,1:T(8,128)(2,1)}, bf16[1792,1,2,512]{3,0,2,1:T(8,128)(2,1)S(1)}, u32[]{:S(2)}) copy-start(bf16[1792,1,2,512]{3,0,2,1:T(8,128)(2,1)S(1)} %copy.66) | copy-start | bytes 11010052
  158.7 7.7 %copy-start.17 = (bf16[1024,1792]{1,0:T(8,128)(2,1)}, bf16[1024,1792]{1,0:T(8,128)(2,1)S(1)}, u32[]{:S(2)}) copy-start(bf16[1024,1792]{1,0:T(8,128)(2,1)S(1)} %get-tuple-element.21) | copy-start | bytes 11010052
  158.7 5.5 %copy-start.21 = (bf16[1024,1792]{1,0:T(8,128)(2,1)S(1)}, bf16[1024,1792]{1,0:T(8,128)(2,1)}, u32[]{:S(2)}) copy-start(bf16[1024,1792]{1,0:T(8,128)(2,1)} %get-tuple-element.23) | copy-start | bytes 11010052
  171.5 1.2 copy-start.1
  171.6 219.6 %reduce-scatter.3.cloned.1.call-start = ((), (), s32[]{:S(2)}) async-start(), calls=%async_computation.7 | async-start | bytes 6193152 | tf_op jit(solution)/shard_map/reduce_scatter | solution.py:69
  206.2 2.7 copy-start.12
  208.9 8.7 %copy-start.7 = (bf16[1792,1,2,512]{3,0,2,1:T(8,128)(2,1)}, bf16[1792,1,2,512]{3,0,2,1:T(8,128)(2,1)S(1)}, u32[]{:S(2)}) copy-start(bf16[1792,1,2,512]{3,0,2,1:T(8,128)(2,1)S(1)} %copy.67) | copy-start | bytes 11010052
  227.2 7.7 %copy-start.19 = (bf16[1024,1792]{1,0:T(8,128)(2,1)}, bf16[1024,1792]{1,0:T(8,128)(2,1)S(1)}, u32[]{:S(2)}) copy-start(bf16[1024,1792]{1,0:T(8,128)(2,1)S(1)} %get-tuple-element.18) | copy-start | bytes 11010052
  227.2 5.5 %copy-start.22 = (bf16[1024,1792]{1,0:T(8,128)(2,1)S(1)}, bf16[1024,1792]{1,0:T(8,128)(2,1)}, u32[]{:S(2)}) copy-start(bf16[1024,1792]{1,0:T(8,128)(2,1)} %get-tuple-element.20) | copy-start | bytes 11010052
  239.9 1.3 copy-start.3
  248.2 5.7 %copy-start.10 = (f32[1024,512]{0,1:T(8,128)S(1)}, f32[1024,512]{0,1:T(8,128)}, u32[]{:S(2)}) copy-start(f32[1024,512]{0,1:T(8,128)} %copy.54) | copy-start | bytes 6291460
  259.1 4.8 %copy-start.8 = (bf16[1792,1,2,512]{3,0,2,1:T(8,128)(2,1)S(1)}, bf16[1792,1,2,512]{3,0,2,1:T(8,128)(2,1)}, u32[]{:S(2)}) copy-start(bf16[1792,1,2,512]{3,0,2,1:T(8,128)(2,1)} %copy-done.7) | copy-start | bytes 11010052
  259.1 4.8 %copy-start.23 = (bf16[1024,1792]{1,0:T(8,128)(2,1)S(1)}, bf16[1024,1792]{1,0:T(8,128)(2,1)}, u32[]{:S(2)}) copy-start(bf16[1024,1792]{1,0:T(8,128)(2,1)} %get-tuple-element.20) | copy-start | bytes 11010052
  263.9 2.1 copy-start.6
  264.0 3.2 copy-start.18
  267.1 2.1 copy-start.20
  273.1 44.8 %all-to-all-start.2 = ((bf16[2,16,64,513]{3,2,0,1:T(8,128)(2,1)}), bf16[2,16,64,513]{3,2,0,1:T(8,128)(2,1)S(1)}, u32[]{:S(2)}, u32[]{:S(2)}) async-start(bf16[2,16,64,513]{3,2,0,1:T(8,128)(2,1)} %pad_maximum_fusion.3), calls=%async_computation.2 | async-start | bytes 5242880 | tf_op jit(solution)/shard_map/all_to_all | solution.py:16
  317.9 1.5 copy-start
  331.8 9.0 %slice-start = ((bf16[2,16,64,513]{3,2,0,1:T(8,128)(2,1)}), bf16[2,16,64,1]{3,2,0,1:T(8,128)(2,1)S(1)}, s32[]{:S(2)}) async-start(bf16[2,16,64,513]{3,2,0,1:T(8,128)(2,1)} %copy-done), calls=%async_computation.9 | async-start | bytes 1048576 | tf_op jit(solution)/shard_map/split | solution.py:17
Sparse Core Ops, SparseCore 0:
  11.1 101.8 all-gather.4
  115.4 79.2 all-gather.2
  198.6 91.2 reduce-scatter.4
  293.7 97.4 reduce-scatter.2
where the time goes:
time: 410 us; the launch traced here: 403 us
  local copies, waits for them, and re-layouts  138 us (34%)
  waiting for transfers between devices  132 us (32%)
  matrix products  77.4 us (19%)
  other arithmetic  23.1 us (6%)
  starting transfers between devices  17.9 us (4%)
  between operations  14.7 us (4%)
    all_to_all x2, waiting for transfers between devices, side_by_side(): lax.all_to_all(both, axis, split_axis=split_dim, concat_axis=concat_dim,...  75.3 us
    dot_general x6, matrix products, contract_last(): lax.dot_general(former, latter, (((1,), (1,)), ((), ())), preferred_eleme...  36.4 us
    reduce_scatter x2, waiting for transfers between devices, reduce_grads(): lax.psum_scatter(jnp.concatenate([jnp.stack([gate_term, up_term], axis=1)...  34.6 us
    scatter x2, local copies, waits for them, and re-layouts, spread(): jnp.zeros((buffer_rows, DS), jnp.bfloat16).at[flat_place].set(doubled)  22.1 us
    all_gather x2, waiting for transfers between devices, rows_first(): filled = lax.all_gather(both, axis, axis=0, tiled=True)  21.6 us
    reshape x4, local copies, waits for them, and re-layouts, rows_first(): b.reshape(-1, *t.shape[1:])  20.4 us
    scatter x1, local copies, waits for them, and re-layouts, body(): jnp.zeros((buffer_rows,), jnp.bfloat16).at[flat_place]  14.6 us
    gather x1, local copies, waits for them, and re-layouts, body(): returned_router.reshape(buffer_rows)[flat_place].reshape(token_count, H, 2)  13.1 us
  transfers between devices with their start and end apart: 7, of which 4 were waited for; matrix products, arithmetic and copies ran while one was open for 55% of the time, Pallas kernels for 0%

commit v1 on v0

--- a/solution.py
+++ b/solution.py
@@ -24,7 +24,9 @@
     turned = [jnp.moveaxis(a, dim, 0) for a, dim in zip(arrays, dims)]
     widths = [t[0].size for t in turned]
     both = jnp.concatenate([t.reshape(-1, w) for t, w in zip(turned, widths)], axis=1)
-    filled = lax.all_gather(both, axis, axis=0, tiled=True)
+    filled = jnp.concatenate(
+        lax.all_to_all(jnp.stack([both] * lax.axis_size(axis)), axis, 0, 0), axis=0
+    )
     tiles = jnp.split(filled, [sum(widths[:k]) for k in range(1, len(widths))], axis=1)
     return tuple(
         (

time: 410 us -> 535 us (1.30)
  waiting for transfers between devices: 132 us -> 247 us
  starting transfers between devices: 17.9 us -> 28 us
    all_to_all x0 -> x2, waiting for transfers between devices: none -> 164 us  [rows_first(): lax.all_to_all(jnp.stack([both] * lax.axis_size(axis)), axis, 0, 0)]
    reduce_scatter x2, waiting for transfers between devices: 34.6 us -> 0.02 us  [reduce_grads(): lax.psum_scatter(jnp.concatenate([jnp.stack([gate_term, up_term], axis=1)...]
    all_gather x2 -> x0, waiting for transfers between devices: 21.6 us -> none  [rows_first(): filled = lax.all_gather(both, axis, axis=0, tiled=True)]
    reshape x4 -> x0, local copies, waits for them, and re-layouts: 20.4 us -> none  [rows_first(): b.reshape(-1, *t.shape[1:])]
    split x2 -> x4, local copies, waits for them, and re-layouts: 8.39 us -> 21.1 us  [rows_first(): jnp.split(filled, [sum(widths[:k]) for k in range(1, len(widths))], axis=1)]
    all_to_all x0 -> x2, starting transfers between devices: none -> 11.7 us  [rows_first(): lax.all_to_all(jnp.stack([both] * lax.axis_size(axis)), axis, 0, 0)]
    all_to_all x2, waiting for transfers between devices: 75.3 us -> 82.8 us  [side_by_side(): lax.all_to_all(both, axis, split_axis=split_dim, concat_axis=concat_dim,...]
    another operation x0 -> x2, local copies, waits for them, and re-layouts: none -> 5.68 us  [rows_first(): jnp.stack([both] * lax.axis_size(axis))]
  transfers between devices with their start and end apart: 7 -> 7, of which waited for: 4 -> 4; matrix products, arithmetic and copies ran while one was open for 55% -> 30% of each run, Pallas kernels for 0% -> 0%
where the time goes in v1:
time: 535 us; the launch traced here: 526 us
  waiting for transfers between devices  247 us (46%)
  local copies, waits for them, and re-layouts  138 us (26%)
  matrix products  77.9 us (15%)
  starting transfers between devices  28 us (5%)
  other arithmetic  20.4 us (4%)
  between operations  15 us (3%)
    all_to_all x2, waiting for transfers between devices, rows_first(): lax.all_to_all(jnp.stack([both] * lax.axis_size(axis)), axis, 0, 0)  164 us
    all_to_all x2, waiting for transfers between devices, side_by_side(): lax.all_to_all(both, axis, split_axis=split_dim, concat_axis=concat_dim,...  82.8 us
    dot_general x6, matrix products, contract_last(): lax.dot_general(former, latter, (((1,), (1,)), ((), ())), preferred_eleme...  36.6 us
    scatter x2, local copies, waits for them, and re-layouts, spread(): jnp.zeros((buffer_rows, DS), jnp.bfloat16).at[flat_place].set(doubled)  22.1 us
    split x4, local copies, waits for them, and re-layouts, rows_first(): jnp.split(filled, [sum(widths[:k]) for k in range(1, len(widths))], axis=1)  21.1 us
    scatter x1, local copies, waits for them, and re-layouts, body(): jnp.zeros((buffer_rows,), jnp.bfloat16).at[flat_place]  14.8 us
    gather x1, local copies, waits for them, and re-layouts, body(): returned_router.reshape(buffer_rows)[flat_place].reshape(token_count, H, 2)  13.1 us
    all_to_all x2, starting transfers between devices, rows_first(): lax.all_to_all(jnp.stack([both] * lax.axis_size(axis)), axis, 0, 0)  11.7 us
  transfers between devices with their start and end apart: 7, of which 4 were waited for; matrix products, arithmetic and copies ran while one was open for 30% of the time, Pallas kernels for 0%

profile of v1, /device:TPU:0, one launch (start us, length us, event | category | flops | bytes accessed | tf_op | source)
XLA Modules:
  0.0 525.6 jit_solution(11343858517513910182)
XLA Ops:
  12.3 2.2 reshape.332
  14.7 10.6 %scatter_custom_fusion.2 = bf16[2048,512]{1,0:T(8,128)(2,1)S(1)} fusion(s32[2048]{0:T(1024)S(1)} %bitcast.162, bf16[2048,512]{1,0:T(8,128)(2,1)} %reshape.332, bf16[]{:T(256)} %constant.31.clone.1), kind=kCustom, calls=%fused_computation.57 | custom fusion | bytes 2097664 | tf_op jit(solution)/shard_map/scatter | solution.py:109
  26.8 6.5 %all-to-all-start.2 = ((bf16[2,16,64,512]{3,2,0,1:T(8,128)(2,1)}), bf16[2,16,64,512]{3,2,0,1:T(8,128)(2,1)S(1)}, u32[]{:S(2)}, u32[]{:S(2)}) async-start(bf16[2,16,64,512]{3,2,0,1:T(8,128)(2,1)} %copy.68), calls=%async_computation.2 | async-start | bytes 4194304 | tf_op jit(solution)/shard_map/all_to_all | solution.py:118
  33.9 14.8 %scatter_custom_fusion.1 = bf16[2048]{0:T(1024)(128)(2,1)S(1)} fusion(s32[2048]{0:T(1024)S(1)} %bitcast.163, bf16[2048]{0:T(1024)(128)(2,1)S(1)} %reshape.324, bf16[]{:T(256)} %constant.31.clone.1), kind=kCustom, calls=%fused_computation.86 | custom fusion | bytes 4098 | tf_op jit(solution)/shard_map/scatter | solution.py:115
  52.0 2.4 broadcast_in_dim.33
  54.5 4.2 reshape.316
  58.6 11.5 %scatter_custom_fusion = bf16[2048,512]{1,0:T(8,128)(2,1)} fusion(s32[2048]{0:T(1024)S(1)} %bitcast.164, bf16[2048,512]{1,0:T(8,128)(2,1)} %reshape.316, bf16[]{:T(256)} %constant.31.clone.1), kind=kCustom, calls=%fused_computation.59 | custom fusion | bytes 2097664 | tf_op jit(solution)/shard_map/scatter | solution.py:109
  75.2 5.7 %all-to-all-start = ((bf16[2,16,64,513]{3,2,0,1:T(8,128)(2,1)}), bf16[2,16,64,513]{3,2,0,1:T(8,128)(2,1)S(1)}, u32[]{:S(2)}, u32[]{:S(2)}) async-start(bf16[2,16,64,513]{3,2,0,1:T(8,128)(2,1)} %copy.65), calls=%async_computation | async-start | bytes 5242880 | tf_op jit(solution)/shard_map/all_to_all | solution.py:16
  82.5 31.9 %all-to-all-done = bf16[2,16,64,513]{3,2,0,1:T(8,128)(2,1)S(1)} async-done(((bf16[2,16,64,513]{3,2,0,1:T(8,128)(2,1)}), bf16[2,16,64,513]{3,2,0,1:T(8,128)(2,1)S(1)}, u32[]{:S(2)}, u32[]{:S(2)}) %all-to-all-start) | async-done | bytes 2101280 | tf_op jit(solution)/shard_map/all_to_all | solution.py:16
  114.4 2.8 stack.32
  117.2 6.6 %all-to-all-start.1 = ((bf16[8,224,1536]{2,1,0:T(8,128)(2,1)}), bf16[8,224,1536]{2,1,0:T(8,128)(2,1)}, u32[]{:S(2)}, u32[]{:S(2)}) async-start(bf16[8,224,1536]{2,1,0:T(8,128)(2,1)} %stack.32), calls=%async_computation.1 | async-start | bytes 11010048 | tf_op jit(solution)/shard_map/all_to_all | solution.py:28
  123.9 3.1 fusion.32
  129.9 70.8 %all-to-all-done.1 = bf16[8,224,1536]{2,1,0:T(8,128)(2,1)} async-done(((bf16[8,224,1536]{2,1,0:T(8,128)(2,1)}), bf16[8,224,1536]{2,1,0:T(8,128)(2,1)}, u32[]{:S(2)}, u32[]{:S(2)}) %all-to-all-start.1) | async-done | bytes 5505056 | tf_op jit(solution)/shard_map/all_to_all | solution.py:28
  200.7 4.2 split.27
  204.9 6.3 %copy.69 = bf16[1792,1024]{0,1:T(8,128)(2,1)} copy(bf16[1792,1024]{1,0:T(8,128)(2,1)} %split.27) | data formatting | bytes 7340032 | tf_op jit(solution)/shard_map/split | solution.py:30
  211.3 3.7 fusion.20
  215.1 5.0 fusion.9
  220.0 9.5 %multiply_convert_fusion.5 = (bf16[1024,1792]{1,0:T(8,128)(2,1)}, bf16[1024,1792]{1,0:T(8,128)(2,1)}, bf16[1024,1792]{1,0:T(8,128)(2,1)S(1)}) fusion(f32[1024,1792]{1,0:T(8,128)S(1)} %fusion.20, f32[1024,1792]{1,0:T(8,128)} %fusion.9, bf16[1024,512]{1,0:T(8,128)(2,1)S(1)} %bitcast.159, bf16[1,2,1792,512]{2,3,1,0:T(8,128)(2,1)S(1)} %bitcast.142), kind=kOutput, calls=%fused_computation.12 | convolution fusion | flops 1906573312 | bytes 28573696 | tf_op jit(solution)/shard_map/dot_general | solution.py:40
  229.6 5.5 %fusion.4 = bf16[1792,1,512]{2,0,1:T(8,128)(2,1)S(1)} fusion(bf16[1024,1792]{1,0:T(8,128)(2,1)} %get-tuple-element.23, bf16[1024,512]{1,0:T(8,128)(2,1)S(1)} %multiply_convert_fusion.7), kind=kOutput, calls=%fused_computation.25 | convolution fusion | flops 1879965696 | bytes 6553600 | tf_op jit(solution)/shard_map/rf,rd->fd/dot_general | solution.py:75
  235.1 2.1 fusion.2
  237.3 2.1 fusion.3
  239.4 2.9 pad_maximum_fusion
  244.0 2.9 stack.68
  246.8 5.1 all-to-all-start.3
  252.3 93.0 %all-to-all-done.3 = bf16[8,224,1536]{2,1,0:T(8,128)(2,1)} async-done(((bf16[8,224,1536]{2,1,0:T(8,128)(2,1)}), bf16[8,224,1536]{2,1,0:T(8,128)(2,1)}, u32[]{:S(2)}, u32[]{:S(2)}) %all-to-all-start.3) | async-done | bytes 5505056 | tf_op jit(solution)/shard_map/all_to_all | solution.py:28
  345.3 4.4 split.29
  349.6 6.1 %copy.74 = bf16[1792,1024]{0,1:T(8,128)(2,1)} copy(bf16[1792,1024]{1,0:T(8,128)(2,1)} %split.29) | data formatting | bytes 7340032 | tf_op jit(solution)/shard_map/split | solution.py:30
  355.8 3.7 fusion.17
  359.6 5.0 fusion.13
  364.5 9.6 %multiply_convert_fusion.3 = (bf16[1024,1792]{1,0:T(8,128)(2,1)}, bf16[1024,1792]{1,0:T(8,128)(2,1)}, bf16[1024,1792]{1,0:T(8,128)(2,1)S(1)}) fusion(f32[1024,1792]{1,0:T(8,128)S(1)} %fusion.17, f32[1024,1792]{1,0:T(8,128)} %fusion.13, bf16[1024,512]{1,0:T(8,128)(2,1)S(1)} %bitcast.155, bf16[1,2,1792,512]{2,3,1,0:T(8,128)(2,1)S(1)} %bitcast.145), kind=kOutput, calls=%fused_computation.8 | convolution fusion | flops 1906573312 | bytes 28573696 | tf_op jit(solution)/shard_map/dot_general | solution.py:40
  374.1 5.5 %fusion.7 = bf16[1792,1,512]{2,0,1:T(8,128)(2,1)S(1)} fusion(bf16[1024,1792]{1,0:T(8,128)(2,1)} %get-tuple-element.26, bf16[1024,512]{1,0:T(8,128)(2,1)S(1)} %multiply_convert_fusion.6), kind=kOutput, calls=%fused_computation.28 | convolution fusion | flops 1879965696 | bytes 6553600 | tf_op jit(solution)/shard_map/rf,rd->fd/dot_general | solution.py:75
  379.7 2.1 fusion.5
  381.8 2.1 fusion.6
  383.9 3.0 pad_maximum_fusion.1
  389.8 2.9 copy.79
  393.0 2.0 copy.80
  395.1 5.5 %multiply_reduce_fusion.1 = bf16[1024]{0:T(1024)(128)(2,1)S(1)} fusion(f32[1024,512]{0,1:T(8,128)} %copy.79, bf16[1024,1792]{1,0:T(8,128)(2,1)} %get-tuple-element.23, bf16[1792,1536]{1,0:T(8,128)(2,1)} %bitcast.5), kind=kOutput, calls=%fused_computation.32 | convolution fusion | flops 1880095744 | bytes 7604224 | tf_op jit(solution)/shard_map/dot_general | solution.py:51
  400.6 4.7 multiply_reduce_fusion
  405.8 5.3 %fusion.8 = f32[1024,512]{1,0:T(8,128)S(1)} fusion(bf16[1024,1792]{1,0:T(8,128)(2,1)} %copy-done.17, bf16[1,2,1792,512]{2,3,1,0:T(8,128)(2,1)} %bitcast.140), kind=kOutput, calls=%fused_computation.41 | convolution fusion | flops 1879048192 | bytes 7602176 | tf_op jit(solution)/shard_map/dot_general | solution.py:63
  411.2 2.1 fusion.12
  414.3 2.1 add_convert_fusion.1
  416.4 2.1 add_convert_fusion
  420.5 4.0 all-to-all-start.4
  424.5 50.9 %all-to-all-done.4 = bf16[2,16,64,513]{3,2,0,1:T(8,128)(2,1)S(1)} async-done(((bf16[2,16,64,513]{3,2,0,1:T(8,128)(2,1)}), bf16[2,16,64,513]{3,2,0,1:T(8,128)(2,1)S(1)}, u32[]{:S(2)}, u32[]{:S(2)}) %all-to-all-start.4) | async-done | bytes 2101280 | tf_op jit(solution)/shard_map/all_to_all | solution.py:16
  479.2 13.1 %gather_fusion.1 = bf16[2048]{0:T(1024)(128)(2,1)S(1)} fusion(bf16[2048]{0:T(1024)(128)(2,1)S(1)} %reshape_reshape.8, s32[2048]{0:T(1024)S(1)} %broadcast_clamp_fusion), kind=kCustom, calls=%fused_computation.1 | custom fusion | bytes 16384 | tf_op jit(solution)/shard_map/gather | solution.py:151
  492.3 9.2 %gather_fusion = bf16[2048,512]{1,0:T(8,128)(2,1)} fusion(bf16[2048,512]{1,0:T(8,128)(2,1)S(1)} %bitcast.137, s32[2048]{0:T(1024)S(1)} %broadcast_clamp_fusion), kind=kCustom, calls=%fused_computation | custom fusion | bytes 4202496 | tf_op jit(solution)/shard_map/gather | solution.py:147
  501.5 2.7 reshape.289
  504.3 5.6 %reduce_sum.32 = bf16[1024,512]{1,0:T(8,128)(2,1)S(1)} reduce(bf16[1024,2,512]{2,1,0:T(2,128)(2,1)S(1)} %reshape.289, bf16[]{:T(256)} %constant.31.clone.1), dimensions={1}, to_apply=%region_5.6 | reduce | flops 524288 | bytes 3145730 | tf_op jit(solution)/shard_map/reduce_sum | solution.py:149
  (106 shorter events, 41.1 us)
Async XLA Ops:
  25.3 8.1 %copy-start.16 = (bf16[128,8,2]{0,2,1:T(2,128)(2,1)S(1)}, bf16[128,8,2]{0,2,1:T(2,128)(2,1)}, u32[]{:S(2)}) copy-start(bf16[128,8,2]{0,2,1:T(2,128)(2,1)} %param.11) | copy-start | bytes 12292
  26.8 47.1 %all-to-all-start.2 = ((bf16[2,16,64,512]{3,2,0,1:T(8,128)(2,1)}), bf16[2,16,64,512]{3,2,0,1:T(8,128)(2,1)S(1)}, u32[]{:S(2)}, u32[]{:S(2)}) async-start(bf16[2,16,64,512]{3,2,0,1:T(8,128)(2,1)} %copy.68), calls=%async_computation.2 | async-start | bytes 4194304 | tf_op jit(solution)/shard_map/all_to_all | solution.py:118
  54.5 15.7 %copy-start.9 = (bf16[2,16,64,1]{3,2,1,0:T(8,128)(2,1)S(1)}, bf16[2,16,64,1]{3,2,1,0:T(8,128)(2,1)}, u32[]{:S(2)}) copy-start(bf16[2,16,64,1]{3,2,1,0:T(8,128)(2,1)} %reshape_reshape.9) | copy-start | bytes 12292
  73.9 7.1 %copy-start.14 = (bf16[2,2,224,512]{3,2,1,0:T(8,128)(2,1)S(1)}, bf16[2,2,224,512]{3,2,1,0:T(8,128)(2,1)}, u32[]{:S(2)}) copy-start(bf16[2,2,224,512]{3,2,1,0:T(8,128)(2,1)} %param.12) | copy-start | bytes 2752516
  73.9 1.4 copy-start.4
  75.2 39.1 %all-to-all-start = ((bf16[2,16,64,513]{3,2,0,1:T(8,128)(2,1)}), bf16[2,16,64,513]{3,2,0,1:T(8,128)(2,1)S(1)}, u32[]{:S(2)}, u32[]{:S(2)}) async-start(bf16[2,16,64,513]{3,2,0,1:T(8,128)(2,1)} %copy.65), calls=%async_computation | async-start | bytes 5242880 | tf_op jit(solution)/shard_map/all_to_all | solution.py:16
  81.0 1.4 copy-start.15
  117.2 83.5 %all-to-all-start.1 = ((bf16[8,224,1536]{2,1,0:T(8,128)(2,1)}), bf16[8,224,1536]{2,1,0:T(8,128)(2,1)}, u32[]{:S(2)}, u32[]{:S(2)}) async-start(bf16[8,224,1536]{2,1,0:T(8,128)(2,1)} %stack.32), calls=%async_computation.1 | async-start | bytes 11010048 | tf_op jit(solution)/shard_map/all_to_all | solution.py:28
  123.8 388.6 %reduce-scatter.3.cloned.1.call-start = ((), (), s32[]{:S(2)}) async-start(), calls=%async_computation.7 | async-start | bytes 6193152 | tf_op jit(solution)/shard_map/reduce_scatter | solution.py:71
  128.6 1.0 copy-start.2
  211.3 3.8 copy-start.5
  211.3 3.8 copy-start.13
  229.6 7.7 %copy-start.17 = (bf16[1024,1792]{1,0:T(8,128)(2,1)}, bf16[1024,1792]{1,0:T(8,128)(2,1)S(1)}, u32[]{:S(2)}) copy-start(bf16[1024,1792]{1,0:T(8,128)(2,1)S(1)} %get-tuple-element.24) | copy-start | bytes 11010052
  229.6 5.5 %copy-start.20 = (bf16[1024,1792]{1,0:T(8,128)(2,1)S(1)}, bf16[1024,1792]{1,0:T(8,128)(2,1)}, u32[]{:S(2)}) copy-start(bf16[1024,1792]{1,0:T(8,128)(2,1)} %get-tuple-element.22) | copy-start | bytes 11010052
  242.3 1.0 copy-start.11
  246.8 5.2 copy-start.1
  246.8 98.5 %all-to-all-start.3 = ((bf16[8,224,1536]{2,1,0:T(8,128)(2,1)}), bf16[8,224,1536]{2,1,0:T(8,128)(2,1)}, u32[]{:S(2)}, u32[]{:S(2)}) async-start(bf16[8,224,1536]{2,1,0:T(8,128)(2,1)} %stack.68), calls=%async_computation.3 | async-start | bytes 11010048 | tf_op jit(solution)/shard_map/all_to_all | solution.py:28
  251.9 261.7 %reduce-scatter.5.cloned.1.call-start = ((), (), s32[]{:S(2)}) async-start(), calls=%async_computation.8 | async-start | bytes 6193152 | tf_op jit(solution)/shard_map/reduce_scatter | solution.py:71
  355.8 3.8 copy-start.7
  355.8 3.8 copy-start.12
  374.1 7.7 %copy-start.18 = (bf16[1024,1792]{1,0:T(8,128)(2,1)}, bf16[1024,1792]{1,0:T(8,128)(2,1)S(1)}, u32[]{:S(2)}) copy-start(bf16[1024,1792]{1,0:T(8,128)(2,1)S(1)} %get-tuple-element.27) | copy-start | bytes 11010052
  374.1 5.5 %copy-start.22 = (bf16[1024,1792]{1,0:T(8,128)(2,1)S(1)}, bf16[1024,1792]{1,0:T(8,128)(2,1)}, u32[]{:S(2)}) copy-start(bf16[1024,1792]{1,0:T(8,128)(2,1)} %get-tuple-element.25) | copy-start | bytes 11010052
  386.9 1.2 copy-start.3
  395.1 5.6 %copy-start.10 = (f32[1024,512]{0,1:T(8,128)S(1)}, f32[1024,512]{0,1:T(8,128)}, u32[]{:S(2)}) copy-start(f32[1024,512]{0,1:T(8,128)} %copy.80) | copy-start | bytes 6291460
  405.8 5.3 %copy-start.8 = (bf16[1792,1024]{0,1:T(8,128)(2,1)S(1)}, bf16[1792,1024]{0,1:T(8,128)(2,1)}, u32[]{:S(2)}) copy-start(bf16[1792,1024]{0,1:T(8,128)(2,1)} %copy.74) | copy-start | bytes 11010052
  405.8 5.3 %copy-start.19 = (bf16[1024,1792]{1,0:T(8,128)(2,1)S(1)}, bf16[1024,1792]{1,0:T(8,128)(2,1)}, u32[]{:S(2)}) copy-start(bf16[1024,1792]{1,0:T(8,128)(2,1)} %copy-done.18) | copy-start | bytes 11010052
  411.2 2.1 copy-start.6
  411.2 3.2 copy-start.21
  414.3 2.1 copy-start.23
  420.5 54.9 %all-to-all-start.4 = ((bf16[2,16,64,513]{3,2,0,1:T(8,128)(2,1)}), bf16[2,16,64,513]{3,2,0,1:T(8,128)(2,1)S(1)}, u32[]{:S(2)}, u32[]{:S(2)}) async-start(bf16[2,16,64,513]{3,2,0,1:T(8,128)(2,1)} %pad_maximum_fusion.3), calls=%async_computation.4 | async-start | bytes 5242880 | tf_op jit(solution)/shard_map/all_to_all | solution.py:16
  475.4 1.6 copy-start
  477.4 1.6 slice-start
Sparse Core Ops, SparseCore 0:
  242.5 152.2 reduce-scatter.2
  398.7 110.7 reduce-scatter.4
